TPU v7x, 32 devices: a whole 2x2x4 slice. The times are simulated.
32 devices in a mesh: dp: 8 (over z, core), tp: 4 (over y, x).
Axes of the slice: x: 2, y: 2, z: 4, core: 2. Of those that a mesh axis runs over, the one named last changes fastest.
Arguments:
- tokens: bfloat16 [4096, 4096], P('dp'), may hold values from -6 to 6
- gain: float32 [4096], replicated, may hold values from 0.1 to 1.9
- router: float32 [4096, 8], replicated, may hold values from -0.09375 to 0.09375
- routes: int32 [4096, 2], P('dp'), may hold values from 0 to 7, all different within a row
- w_gate: bfloat16 [2, 4096, 1024], P(None, 'dp', 'tp'), may hold values from -0.125 to 0.125
- w_up: bfloat16 [2, 4096, 1024], P(None, 'dp', 'tp'), may hold values from -0.125 to 0.125
- w_down: bfloat16 [2, 1024, 4096], P(None, 'dp', 'tp'), may hold values from -0.25 to 0.25
Outputs:
- mixed: bfloat16 [4096, 4096], P('dp', 'tp')
Inputs may be any that keep to these rules, and one draw needn't show every extreme that they name: `routes`: each row names two different experts.
All inputs are finite; a program needn't handle non-finite values.
Results may differ from a plain program's by a relative error of at most 0.0065.
Values may be sent and summed in bfloat16 or wider, within the bound.
A program may use at most 64 MiB of HBM per device.

v0:
```python
import functools

import jax
import jax.numpy as jnp
from jax import lax
from jax.experimental import pallas as pl
from jax.experimental.pallas import tpu as pltpu
from jax.sharding import PartitionSpec as P

EPS = 1e-06
ROUTE_SCALE = 2.5
MESH = pl.DeviceIdType.MESH
CORES = 2
PIECES = 4
HOSTED = (0, 1)


def gathered(tokens, gain, router, routes, w_gate, w_up, w_down):
    values = tokens.astype(jnp.float32)
    square = jnp.mean(values * values, axis=-1, keepdims=True)
    normed = (values * lax.rsqrt(square + EPS) * gain).astype(jnp.bfloat16)
    scores = jax.nn.sigmoid(
        jnp.dot(normed.astype(jnp.float32), router, precision=lax.Precision.HIGHEST)
    )
    labels = jnp.arange(router.shape[1], dtype=jnp.int32)
    picked_mask = (routes[:, :, None] == labels[None, None, :]).astype(jnp.float32)
    picked = jnp.sum(picked_mask * scores[:, None, :], axis=-1)
    chosen = jnp.sum(picked_mask, axis=1)
    combine = chosen * scores * ROUTE_SCALE / jnp.sum(picked, axis=-1, keepdims=True)
    held_weights = combine[:, : w_gate.shape[0]]
    full_gate, full_up, full_down = (
        lax.all_gather(w_gate, "dp", axis=1, tiled=True),
        lax.all_gather(w_up, "dp", axis=1, tiled=True),
        lax.all_gather(w_down, "dp", axis=1, tiled=True),
    )
    gate_value = jnp.einsum("td,edf->tef", normed, full_gate, preferred_element_type=jnp.float32)
    up_value = jnp.einsum("td,edf->tef", normed, full_up, preferred_element_type=jnp.float32)
    hidden = (jax.nn.silu(gate_value) * up_value * held_weights[:, :, None]).astype(jnp.bfloat16)
    whole_hidden = lax.all_gather(hidden, "tp", axis=2, tiled=True)
    mixed = jnp.einsum("tef,efd->td", whole_hidden, full_down, preferred_element_type=jnp.float32)
    return mixed.astype(jnp.bfloat16)


def kernel(
    groups, tps, hosted, x_hbm, gain_ref, router_ref, routes_ref, wg_hbm, wu_hbm, wd_hbm, o_ref,
    x, guest, guest_normed, w, dn, hid, guest_hid, comb,
    x_sem, own_sem, recv_sem, in_sem, out_sem, side_sem, hid_send, hid_recv,
    tok_send, tok_recv, back_send, back_recv,
):
    dp, tp = lax.axis_index("dp"), lax.axis_index("tp")
    positions = groups // CORES
    z, core = dp // CORES, dp % CORES
    experts = wg_hbm.shape[0]
    rows = x.shape[0]
    end = jnp.logical_or(z == positions - 1, z == 0)
    out = 2 * (2 * z // positions) - 1

    def at(p):
        return (p * CORES + core, tp)

    inner = at(z - out)
    outer = at(jnp.clip(z + out, 0, positions - 1))
    side = (z * CORES + (1 - core), tp)
    along_x = tp + 1 - 2 * (tp % 2)
    along_y = lax.rem(tp + 2, tps)
    across = lax.rem(along_x + 2, tps)

    load_x = pltpu.make_async_copy(x_hbm, x, x_sem)
    load_x.start()
    order = sorted(range(experts), key=lambda e: e not in hosted)
    chunks = [(m, e) for e in order for m in (0, 1)] + [(2, e) for e in range(experts)]
    everywhere = [k for k, (m, e) in enumerate(chunks) if m == 2 or e not in hosted]
    feeds = [k for k, (m, e) in enumerate(chunks) if m < 2]
    downs = [k for k, (m, e) in enumerate(chunks) if m == 2]

    def source(k):
        m, e = chunks[k]
        return (wg_hbm, wu_hbm, wd_hbm)[m].at[e]

    def slot(k, d):
        m, e = chunks[k]
        return dn.at[e, d] if m == 2 else w.at[m, e, d]

    def copy_own(k):
        return pltpu.make_async_copy(source(k), slot(k, dp), own_sem.at[k])

    for k in range(len(chunks)):
        copy_own(k).start()

    barrier = pltpu.get_barrier_semaphore()
    pl.semaphore_signal(barrier, inc=1, device_id=side, device_id_type=MESH)
    pl.semaphore_signal(barrier, inc=1, device_id=inner, device_id_type=MESH)
    for i in range(1, tps):
        pl.semaphore_signal(
            barrier, inc=1, device_id=(dp, lax.rem(tp + i, tps)), device_id_type=MESH
        )

    @pl.when(jnp.logical_not(end))
    def _():
        pl.semaphore_signal(barrier, inc=1, device_id=outer, device_id_type=MESH)

    pl.semaphore_wait(barrier, tps + 2 - jnp.where(end, 1, 0))

    def send(k, d, src, sem, to):
        return pltpu.make_async_remote_copy(
            src_ref=src, dst_ref=slot(k, d), send_sem=sem.at[k, d // CORES],
            recv_sem=recv_sem.at[k, d], device_id=to, device_id_type=MESH,
        )

    def arrived(k, d):
        send(k, d, slot(k, d), side_sem, side).wait_recv()

    def pass_on(k, p, targets):
        d = p * CORES + core
        arrived(k, d)
        for sem, to in targets:
            send(k, d, slot(k, d), sem, to).start()

    def wait_side(k):
        for p in range(positions):
            arrived(k, p * CORES + (1 - core))
        copy_own(k).wait()

    quarter = rows // tps
    piece = quarter // PIECES

    def token_part(q, p):
        return pl.ds(pl.multiple_of(q * quarter + p * piece, piece), piece)

    def token_copy(src, q, p, kind, to):
        return pltpu.make_async_remote_copy(
            src_ref=src.at[token_part(q, p)], dst_ref=guest.at[token_part(q, p)],
            send_sem=tok_send.at[kind, p], recv_sem=tok_recv.at[q, p],
            device_id=to, device_id_type=MESH,
        )

    def token_arrived(q, p):
        token_copy(guest, q, p, 0, side).wait_recv()

    def norm(src, dst, start, count, steps):
        step = count // steps

        def body(i, _):
            part = pl.ds(pl.multiple_of(start + i * step, step), step)
            v = src[part, :].astype(jnp.float32)
            square = jnp.mean(v * v, axis=-1, keepdims=True)
            dst[part, :] = (v * lax.rsqrt(square + EPS) * gain_ref[...]).astype(jnp.bfloat16)
            return 0

        lax.fori_loop(0, steps, body, 0)

    def norm_quarter(q):
        norm(guest, guest_normed, q * quarter, quarter, 2)

    def score():
        rest = router_ref[...]
        total = jnp.zeros((rows, rest.shape[0]), jnp.float32)
        parts = []
        for _ in range(3):
            part = rest.astype(jnp.bfloat16)
            rest = rest - part.astype(jnp.float32)
            parts.append(part)
        for part in parts[::-1]:
            total += lax.dot_general(
                x[...], part, (((1,), (1,)), ((), ())), preferred_element_type=jnp.float32
            )
        scores = 1.0 / (1.0 + jnp.exp(-total))
        routed = scores.shape[1]
        picks = routes_ref[...].astype(jnp.float32)
        labels = lax.broadcasted_iota(jnp.int32, scores.shape, 1).astype(jnp.float32)
        chosen = jnp.zeros_like(scores)
        for i in range(routes_ref.shape[0]):
            column = jnp.transpose(jnp.broadcast_to(picks[i : i + 1, :], (128, rows)))
            chosen += jnp.where(column[:, :routed] == labels, 1.0, 0.0)
        picked = chosen * scores
        comb[...] = picked * ROUTE_SCALE / jnp.sum(picked, axis=-1, keepdims=True)

    def send_hidden(e, i):
        return pltpu.make_async_remote_copy(
            src_ref=hid.at[e, tp], dst_ref=hid.at[e, tp], send_sem=hid_send.at[e, i - 1],
            recv_sem=hid_recv.at[e, tp],
            device_id=(dp, lax.rem(tp + i, tps)), device_id_type=MESH,
        )

    def share_hidden(e):
        for i in range(1, tps):
            send_hidden(e, i).start()

    def send_back(e):
        return pltpu.make_async_remote_copy(
            src_ref=guest_hid.at[e], dst_ref=hid.at[e, tp], send_sem=back_send.at[e],
            recv_sem=back_recv.at[e], device_id=outer, device_id_type=MESH,
        )

    def expert_hidden(e, src, dst):
        step = rows // 2

        def body(i, _):
            part = pl.ds(pl.multiple_of(i * step, step), step)
            lhs = src[part, :]
            depth = x.shape[1]
            gate = jnp.dot(
                lhs, w[0, e].reshape(depth, w.shape[-1]), preferred_element_type=jnp.float32
            )
            up = jnp.dot(
                lhs, w[1, e].reshape(depth, w.shape[-1]), preferred_element_type=jnp.float32
            )
            dst[part, :] = (gate / (1.0 + jnp.exp(-gate)) * up).astype(jnp.bfloat16)
            return 0

        lax.fori_loop(0, 2, body, 0)

    def own_hidden(e):
        expert_hidden(e, x, hid.at[e, tp])
        share_hidden(e)

    def guest_hidden(e):
        expert_hidden(e, guest_normed, guest_hid.at[e])
        send_back(e).start()

    def sides_of(e):
        for k in feeds:
            if chunks[k][1] == e:
                wait_side(k)

    def down():
        cols = o_ref.shape[1]
        step = cols // 4

        def body(i, _):
            part = pl.ds(pl.multiple_of(i * step, step), step)
            total = None
            for e in range(experts):
                lhs = jnp.concatenate([hid[e, t] for t in range(tps)], axis=1)
                rhs = dn[e, :, :, part].reshape(lhs.shape[1], step)
                term = jnp.dot(lhs, rhs, preferred_element_type=jnp.float32)
                term = term * comb[:, e : e + 1]
                total = term if total is None else total + term
            o_ref[:, part] = total.astype(o_ref.dtype)
            return 0

        lax.fori_loop(0, 4, body, 0)

    to_in, to_out, to_side = (in_sem, inner), (out_sem, outer), (side_sem, side)

    @pl.when(end)
    def _():
        for p in range(PIECES):
            token_copy(x_hbm, tp, p, 0, inner).start()
        for k in range(len(chunks)):
            send(k, dp, source(k), *to_in).start()
        for k in everywhere:
            send(k, dp, source(k), *to_side).start()
        load_x.wait()
        norm(x, x, 0, rows, 8)
        score()
        for j in range(1, positions - 1):
            for k in everywhere:
                pass_on(k, z - j * out, [to_side])
        for e in order:
            if e in hosted:
                send_back(e).wait_recv()
                share_hidden(e)
        for e in order:
            if e not in hosted:
                for k in feeds:
                    if chunks[k][1] == e:
                        pass_on(k, z - (positions - 1) * out, [to_side])
                sides_of(e)
                own_hidden(e)
        for k in downs:
            pass_on(k, z - (positions - 1) * out, [to_side])
        for k in range(len(chunks)):
            if k not in everywhere:
                copy_own(k).wait()

    @pl.when(jnp.logical_not(end))
    def _():
        def beyond(k):
            return [to_out] if k in everywhere else []

        for k in range(len(chunks)):
            send(k, dp, source(k), *to_in).start()
        for k in everywhere:
            send(k, dp, source(k), *to_out).start()
        for k in range(len(chunks)):
            send(k, dp, source(k), *to_side).start()

        def from_outer(k):
            pass_on(k, z + out, [to_in, to_side])

        def from_near(k):
            pass_on(k, z - out, beyond(k) + [to_side])

        def from_far(k):
            pass_on(k, z - 2 * out, beyond(k) + [to_side])

        load_x.wait()
        norm(x, x, 0, rows, 8)
        for p in range(PIECES):
            token_arrived(tp, p)
            token_copy(guest, tp, p, 0, (dp, along_x)).start()
            token_copy(guest, tp, p, 1, (dp, along_y)).start()
            from_near(p)
        norm_quarter(tp)
        for p in range(PIECES):
            token_arrived(along_x, p)
            if p < PIECES // 2:
                token_copy(guest, along_x, p, 2, (dp, along_y)).start()
            token_arrived(along_y, p)
            if p >= PIECES // 2:
                token_copy(guest, along_y, p, 2, (dp, along_x)).start()
            if p == 1:
                score()
                for k in downs:
                    from_near(k)
            if p == 2:
                from_outer(feeds[0])
        from_outer(feeds[1])
        norm_quarter(along_x)
        norm_quarter(along_y)
        from_far(feeds[0])
        from_outer(feeds[2])
        for p in range(PIECES):
            token_arrived(across, p)
        norm_quarter(across)
        from_far(feeds[1])
        from_outer(feeds[3])
        sides_of(order[0])
        guest_hidden(order[0])
        from_outer(downs[0])
        from_far(feeds[2])
        own_hidden(order[0])
        from_outer(downs[1])
        from_far(feeds[3])
        sides_of(order[1])
        if order[1] in hosted:
            guest_hidden(order[1])
        own_hidden(order[1])
        for k in downs:
            from_far(k)

    for k in downs:
        wait_side(k)
    for e in order:
        for i in range(1, tps):
            s = lax.rem(tp + i, tps)
            pltpu.make_async_remote_copy(
                src_ref=hid.at[e, s], dst_ref=hid.at[e, s], send_sem=hid_send.at[e, i - 1],
                recv_sem=hid_recv.at[e, s], device_id=side, device_id_type=MESH,
            ).wait_recv()
    down()

    def sent(k, p, sem):
        d = p * CORES + core
        send(k, d, slot(k, d), sem, side).wait_send()

    for e in range(experts):
        for i in range(1, tps):
            send_hidden(e, i).wait_send()
    for k in range(len(chunks)):
        sent(k, z, in_sem)

    @pl.when(end)
    def _():
        for p in range(PIECES):
            token_copy(x_hbm, tp, p, 0, inner).wait_send()
        for k in everywhere:
            for p in range(positions):
                sent(k, p, side_sem)

    @pl.when(jnp.logical_not(end))
    def _():
        for p in range(PIECES):
            for kind in range(3):
                token_copy(guest, tp, p, kind, side).wait_send()
        for e in hosted:
            send_back(e).wait_send()
        for k in range(len(chunks)):
            sent(k, z + out, in_sem)
            for p in range(positions):
                sent(k, p, side_sem)
        for k in everywhere:
            sent(k, z, out_sem)
            sent(k, z - out, out_sem)
            sent(k, z - 2 * out, out_sem)


def streamed(groups, tps, tokens, gain, router, routes, w_gate, w_up, w_down):
    rows, depth = tokens.shape
    experts, shard, width = w_gate.shape
    down_rows, cols = w_down.shape[1:]
    positions = groups // CORES
    vmem = pl.BlockSpec(memory_space=pltpu.VMEM)
    hbm = pl.BlockSpec(memory_space=pl.ANY)
    chunks = 3 * experts
    dma = pltpu.SemaphoreType.DMA
    return pl.pallas_call(
        functools.partial(kernel, groups, tps, HOSTED),
        out_shape=jax.ShapeDtypeStruct((rows, cols), jnp.bfloat16),
        in_specs=[hbm, vmem, vmem, vmem, hbm, hbm, hbm],
        out_specs=vmem,
        scratch_shapes=[
            pltpu.VMEM((rows, depth), jnp.bfloat16),
            pltpu.VMEM((rows, depth), jnp.bfloat16),
            pltpu.VMEM((rows, depth), jnp.bfloat16),
            pltpu.VMEM((2, experts, groups, shard, width), jnp.bfloat16),
            pltpu.VMEM((experts, groups, down_rows, cols), jnp.bfloat16),
            pltpu.VMEM((experts, tps, rows, width), jnp.bfloat16),
            pltpu.VMEM((experts, rows, width), jnp.bfloat16),
            pltpu.VMEM((rows, router.shape[1]), jnp.float32),
            dma,
            dma((chunks,)),
            dma((chunks, groups)),
            dma((chunks, positions)),
            dma((chunks, positions)),
            dma((chunks, positions)),
            dma((experts, tps - 1)),
            dma((experts, tps)),
            dma((3, PIECES)),
            dma((tps, PIECES)),
            dma((experts,)),
            dma((experts,)),
        ],
        compiler_params=pltpu.CompilerParams(
            collective_id=0, has_side_effects=True, vmem_limit_bytes=60 * 1024 * 1024
        ),
    )(tokens, gain.reshape(1, -1), router.T, routes.T, w_gate, w_up, w_down)


def solution(mesh):
    groups, tps = mesh.shape["dp"], mesh.shape["tp"]
    fits = groups == 4 * CORES and tps == 4
    body = functools.partial(streamed, groups, tps) if fits else gathered
    return jax.shard_map(
        body,
        mesh=mesh,
        in_specs=(
            P("dp", None),
            P(),
            P(),
            P("dp", None),
            P(None, "dp", "tp"),
            P(None, "dp", "tp"),
            P(None, "dp", "tp"),
        ),
        out_specs=P("dp", "tp"),
        check_vma=False,
    )
```

profile of v0, /device:TPU:0, one launch (start us, length us, event | category | flops | bytes accessed | tf_op | source)
XLA Modules:
  0.0 96.7 jit_solution(12134697374242135262)
XLA Ops:
  0.0 94.4 %shard_map.73 = bf16[512,1024]{1,0:T(8,128)(2,1)} custom-call(bf16[512,4096]{1,0:T(8,128)(2,1)} %x_hbm.1, f32[1,4096]{1,0:T(1,128)} %bitcast.4, f32[8,4096]{1,0:T(8,128)} %bitcast.3, s32[2,512]{1,0:T(2,128)} %bitcast.5, bf16[2,512,256]{2,1,0:T(8,128)(2,1)} %wg_hbm.1, bf16[2,512,256]{2,1,0:T(8,128)(2,1)} %wu_hbm.1, bf16[2,128,1024]{2,1,0:T(8,128)(2,1)} %wd_hbm.1), custom_call_target="tpu_custom_call" | custom-call | tf_op jit(solution)/shard_map/pallas_call | solution.py:398
  94.4 2.3 %copy.9 = bf16[512,1024]{1,0:T(8,128)(2,1)} copy(bf16[512,1024]{1,0:T(8,128)(2,1)} %shard_map.73) | data formatting | bytes 2097152
where the time goes:
time: 96.8 us; the launch traced here: 96.7 us
  Pallas kernels  94.4 us (98%)
  local copies, waits for them, and re-layouts  2.26 us (2%)
    pallas_call x1, Pallas kernels, streamed(): pl.pallas_call(functools.partial(kernel, groups, tps, HOSTED), out_shape=...  94.4 us
    unnamed x1, local copies, waits for them, and re-layouts  2.26 us

commit v1 on v0

v1 whole, which is shorter than its diff:
```python
import functools

import jax
import jax.numpy as jnp
from jax import lax
from jax.experimental import pallas as pl
from jax.experimental.pallas import tpu as pltpu
from jax.sharding import PartitionSpec as P

EPS = 1e-06
ROUTE_SCALE = 2.5
MESH = pl.DeviceIdType.MESH
CORES = 2
PIECES = 8
CUTS = 2
HALVES = 2


def gathered(tokens, gain, router, routes, w_gate, w_up, w_down):
    values = tokens.astype(jnp.float32)
    square = jnp.mean(values * values, axis=-1, keepdims=True)
    normed = (values * lax.rsqrt(square + EPS) * gain).astype(jnp.bfloat16)
    scores = jax.nn.sigmoid(
        jnp.dot(normed.astype(jnp.float32), router, precision=lax.Precision.HIGHEST)
    )
    labels = jnp.arange(router.shape[1], dtype=jnp.int32)
    picked_mask = (routes[:, :, None] == labels[None, None, :]).astype(jnp.float32)
    picked = jnp.sum(picked_mask * scores[:, None, :], axis=-1)
    chosen = jnp.sum(picked_mask, axis=1)
    combine = chosen * scores * ROUTE_SCALE / jnp.sum(picked, axis=-1, keepdims=True)
    held_weights = combine[:, : w_gate.shape[0]]
    full_gate, full_up, full_down = (
        lax.all_gather(w_gate, "dp", axis=1, tiled=True),
        lax.all_gather(w_up, "dp", axis=1, tiled=True),
        lax.all_gather(w_down, "dp", axis=1, tiled=True),
    )
    gate_value = jnp.einsum("td,edf->tef", normed, full_gate, preferred_element_type=jnp.float32)
    up_value = jnp.einsum("td,edf->tef", normed, full_up, preferred_element_type=jnp.float32)
    hidden = (jax.nn.silu(gate_value) * up_value * held_weights[:, :, None]).astype(jnp.bfloat16)
    whole_hidden = lax.all_gather(hidden, "tp", axis=2, tiled=True)
    mixed = jnp.einsum("tef,efd->td", whole_hidden, full_down, preferred_element_type=jnp.float32)
    return mixed.astype(jnp.bfloat16)


def kernel(
    groups, tps, x_hbm, gain_hbm, router_hbm, routes_hbm, wg_hbm, wu_hbm, wd_hbm, o_ref,
    x, guest, guest_normed, w, dn, hid, guest_hid, comb, acc, gain_ref, router_ref, routes_ref,
    x_sem, own_sem, recv_sem, in_sem, out_sem, side_sem, hid_send, hid_recv,
    tok_send, tok_recv, back_send, back_recv,
):
    dp, tp = lax.axis_index("dp"), lax.axis_index("tp")
    positions = groups // CORES
    z, core = dp // CORES, dp % CORES
    experts = wg_hbm.shape[0]
    rows = x.shape[0]
    half = wg_hbm.shape[2] // HALVES
    end = jnp.logical_or(z == positions - 1, z == 0)
    out = 2 * (2 * z // positions) - 1

    def at(p):
        return (p * CORES + core, tp)

    inner = at(z - out)
    outer = at(jnp.clip(z + out, 0, positions - 1))
    side = (z * CORES + (1 - core), tp)
    along_x = tp + 1 - 2 * (tp % 2)
    along_y = lax.rem(tp + 2, tps)
    across = lax.rem(along_x + 2, tps)
    far = jnp.where(2 * z < positions, positions - 1, 0)
    others = [lax.rem(far + i, positions) for i in range(1, positions)]

    barrier = pltpu.get_barrier_semaphore()
    pl.semaphore_signal(barrier, inc=1, device_id=side, device_id_type=MESH)
    pl.semaphore_signal(barrier, inc=1, device_id=inner, device_id_type=MESH)
    for i in range(1, tps):
        pl.semaphore_signal(
            barrier, inc=1, device_id=(dp, lax.rem(tp + i, tps)), device_id_type=MESH
        )

    @pl.when(jnp.logical_not(end))
    def _():
        pl.semaphore_signal(barrier, inc=1, device_id=outer, device_id_type=MESH)

    loads = [
        pltpu.make_async_copy(src, dst, x_sem.at[i])
        for i, (src, dst) in enumerate(
            [(x_hbm, x), (gain_hbm, gain_ref), (router_hbm, router_ref), (routes_hbm, routes_ref)]
        )
    ]
    for load in loads:
        load.start()
    units = experts * HALVES
    feeds = list(range(2 * units))
    downs = list(range(2 * units, 2 * units + experts * CUTS))
    pieces = feeds + downs
    cut = wd_hbm.shape[1] // CUTS

    def source(k):
        if k < 2 * units:
            e, h = divmod(k // 2, HALVES)
            return (wg_hbm, wu_hbm)[k % 2].at[e, :, pl.ds(h * half, half)]
        e, r = divmod(k - 2 * units, CUTS)
        return wd_hbm.at[e, pl.ds(r * cut, cut), :]

    def slot(k, d):
        if k < 2 * units:
            return w.at[k // 2, k % 2, d]
        e, r = divmod(k - 2 * units, CUTS)
        return dn.at[e, d, pl.ds(r * cut, cut), :]

    def copy_own(k):
        return pltpu.make_async_copy(source(k), slot(k, dp), own_sem.at[k])

    for k in downs:
        copy_own(k).start()

    @pl.when(jnp.logical_not(end))
    def _():
        for k in feeds:
            copy_own(k).start()

    pl.semaphore_wait(barrier, tps + 2 - jnp.where(end, 1, 0))

    def send(k, d, src, sem, to):
        return pltpu.make_async_remote_copy(
            src_ref=src, dst_ref=slot(k, d), send_sem=sem.at[k, d // CORES],
            recv_sem=recv_sem.at[k, d], device_id=to, device_id_type=MESH,
        )

    def arrived(k, d):
        send(k, d, slot(k, d), side_sem, side).wait_recv()

    def pass_on(k, p, targets):
        d = p * CORES + core
        arrived(k, d)
        for sem, to in targets:
            send(k, d, slot(k, d), sem, to).start()

    def from_side(k, p):
        arrived(k, p * CORES + (1 - core))

    quarter = rows // tps
    piece = quarter // PIECES

    def token_part(q, p):
        return pl.ds(pl.multiple_of(q * quarter + p * piece, piece), piece)

    def token_copy(src, q, p, kind, to):
        return pltpu.make_async_remote_copy(
            src_ref=src.at[token_part(q, p)], dst_ref=guest.at[token_part(q, p)],
            send_sem=tok_send.at[kind, p], recv_sem=tok_recv.at[q, p],
            device_id=to, device_id_type=MESH,
        )

    def token_arrived(q, p):
        token_copy(guest, q, p, 0, side).wait_recv()

    def norm(src, dst, start, count, steps):
        step = count // steps

        def body(i, _):
            part = pl.ds(pl.multiple_of(start + i * step, step), step)
            v = src[part, :].astype(jnp.float32)
            square = jnp.mean(v * v, axis=-1, keepdims=True)
            dst[part, :] = (v * lax.rsqrt(square + EPS) * gain_ref[...]).astype(jnp.bfloat16)
            return 0

        lax.fori_loop(0, steps, body, 0)

    def norm_quarter(q):
        norm(guest, guest_normed, q * quarter, quarter, 2)

    def score():
        rest = router_ref[...]
        routed = rest.shape[0]
        parts = []
        for _ in range(3):
            part = rest.astype(jnp.bfloat16).astype(jnp.float32)
            rest = rest - part
            parts.append(part)
        parts.append(jnp.zeros_like(rest))
        stacked = jnp.concatenate(parts, axis=0).astype(jnp.bfloat16)
        sums = lax.dot_general(
            x[...], stacked, (((1,), (1,)), ((), ())), preferred_element_type=jnp.float32
        )
        total = sums[:, 2 * routed : 3 * routed] + sums[:, routed : 2 * routed] + sums[:, :routed]
        scores = 1.0 / (1.0 + jnp.exp(-total))
        picks = routes_ref[...].astype(jnp.float32)
        labels = lax.broadcasted_iota(jnp.int32, scores.shape, 1).astype(jnp.float32)
        chosen = jnp.zeros_like(scores)
        for i in range(routes_ref.shape[0]):
            column = jnp.transpose(jnp.broadcast_to(picks[i : i + 1, :], (128, rows)))
            chosen += jnp.where(column[:, :routed] == labels, 1.0, 0.0)
        picked = chosen * scores
        comb[...] = picked * ROUTE_SCALE / jnp.sum(picked, axis=-1, keepdims=True)

    def send_hidden(q, i):
        return pltpu.make_async_remote_copy(
            src_ref=hid.at[q, tp], dst_ref=hid.at[q, tp], send_sem=hid_send.at[q, i - 1],
            recv_sem=hid_recv.at[q, tp],
            device_id=(dp, lax.rem(tp + i, tps)), device_id_type=MESH,
        )

    def share_hidden(q):
        for i in range(1, tps):
            send_hidden(q, i).start()

    def hidden_arrived(q):
        for i in range(1, tps):
            s = lax.rem(tp + i, tps)
            pltpu.make_async_remote_copy(
                src_ref=hid.at[q, s], dst_ref=hid.at[q, s], send_sem=hid_send.at[q, i - 1],
                recv_sem=hid_recv.at[q, s], device_id=side, device_id_type=MESH,
            ).wait_recv()

    def send_back(q):
        return pltpu.make_async_remote_copy(
            src_ref=guest_hid.at[q], dst_ref=hid.at[q, tp], send_sem=back_send.at[q],
            recv_sem=back_recv.at[q], device_id=outer, device_id_type=MESH,
        )

    def unit_hidden(q, src, dst):
        depth = x.shape[1]
        step = rows // 2

        def body(i, _):
            part = pl.ds(pl.multiple_of(i * step, step), step)
            weights = jnp.concatenate(
                [w[q, 0].reshape(depth, half), w[q, 1].reshape(depth, half)], axis=1
            )
            both = jnp.dot(src[part, :], weights, preferred_element_type=jnp.float32)
            gate, up = both[:, :half], both[:, half:]
            dst[part, :] = (gate / (1.0 + jnp.exp(-gate)) * up).astype(jnp.bfloat16)
            return 0

        lax.fori_loop(0, 2, body, 0)

    def own_hidden(q):
        unit_hidden(q, x, hid.at[q, tp])
        share_hidden(q)

    def guest_hidden(q):
        unit_hidden(q, guest_normed, guest_hid.at[q])
        send_back(q).start()

    def sides_of(q):
        for k in (2 * q, 2 * q + 1):
            for p in range(positions):
                from_side(k, p)
            copy_own(k).wait()

    def down(terms, first, last):
        cols = o_ref.shape[1]
        step = cols // 4

        def body(i, _):
            part = pl.ds(pl.multiple_of(i * step, step), step)
            total = None if first else acc[:, part]
            for e, spots in terms:
                lhs = jnp.concatenate(
                    [hid[e * HALVES + h, t] for t in spots for h in range(HALVES)], axis=1
                )
                rhs = jnp.concatenate(
                    [
                        dn[e, pl.ds(t * CORES, CORES), :, part].reshape(HALVES * half, step)
                        for t in spots
                    ],
                    axis=0,
                )
                term = jnp.dot(lhs, rhs, preferred_element_type=jnp.float32)
                term = term * comb[:, e : e + 1]
                total = term if total is None else total + term
            if last:
                o_ref[:, part] = total.astype(o_ref.dtype)
            else:
                acc[:, part] = total
            return 0

        lax.fori_loop(0, 4, body, 0)

    def down_near(e):
        for q in range(e * HALVES, (e + 1) * HALVES):
            hidden_arrived(q)
        for k in downs[e * CUTS : (e + 1) * CUTS]:
            for p in others:
                from_side(k, p)
            copy_own(k).wait()
        down([(e, others)], e == 0, False)

    to_in, to_out, to_side = (in_sem, inner), (out_sem, outer), (side_sem, side)

    @pl.when(end)
    def _():
        for p in range(PIECES):
            token_copy(x_hbm, tp, p, 0, inner).start()
        for k in pieces:
            send(k, dp, source(k), *to_in).start()
        for k in downs:
            send(k, dp, source(k), *to_side).start()
        for load in loads:
            load.wait()
        norm(x, x, 0, rows, 8)
        score()
        for j in range(1, positions - 1):
            for k in downs:
                pass_on(k, z - j * out, [to_side])
        for q in range(units):
            send_back(q).wait_recv()
            share_hidden(q)
            if q == units - 2:
                down_near(0)
        for k in downs[:-1]:
            pass_on(k, far, [to_side])
        down_near(1)
        pass_on(downs[-1], far, [to_side])

    @pl.when(jnp.logical_not(end))
    def _():
        for k in pieces:
            send(k, dp, source(k), *to_in).start()
        for k in downs:
            send(k, dp, source(k), *to_out).start()
        for k in pieces:
            send(k, dp, source(k), *to_side).start()

        def beyond(k):
            return [to_out] if k in downs else []

        def from_outer(k):
            pass_on(k, z + out, [to_in, to_side])

        def from_near(k):
            pass_on(k, z - out, beyond(k) + [to_side])

        def from_far(k):
            pass_on(k, far, beyond(k) + [to_side])

        for load in loads:
            load.wait()
        norm(x, x, 0, rows, 8)
        for p in range(PIECES):
            token_arrived(tp, p)
            token_copy(guest, tp, p, 0, (dp, along_x)).start()
            token_copy(guest, tp, p, 1, (dp, along_y)).start()
            from_near(feeds[p])
            if p == 1:
                score()
        for p in range(PIECES // 2):
            token_arrived(along_x, p)
            token_copy(guest, along_x, p, 2, (dp, along_y)).start()
            token_arrived(along_y, p + PIECES // 2)
            token_copy(guest, along_y, p + PIECES // 2, 2, (dp, along_x)).start()
        norm_quarter(tp)
        for i in range(4):
            from_outer(feeds[i])
            from_near(downs[i])
            if i == 0:
                for p in range(PIECES // 2):
                    token_arrived(along_x, p + PIECES // 2)
                    token_arrived(along_y, p)
                norm_quarter(along_x)
            if i == 1:
                norm_quarter(along_y)
        from_far(feeds[0])
        from_outer(feeds[4])
        for p in range(PIECES):
            token_arrived(across, p)
        norm_quarter(across)
        from_far(feeds[1])
        from_outer(feeds[5])
        late = feeds[6:] + downs
        for q in range(units):
            sides_of(q)
            guest_hidden(q)
            own_hidden(q)
            for i in (2 * q, 2 * q + 1):
                if i + 2 < len(feeds):
                    from_far(feeds[i + 2])
                if i < len(late):
                    from_outer(late[i])
        down_near(0)
        for k in downs[:-1]:
            from_far(k)
        down_near(1)
        from_far(downs[-1])

    for k in downs:
        from_side(k, far)
    down([(e, [far]) for e in range(experts)], False, True)

    def sent(k, p, sem):
        d = p * CORES + core
        send(k, d, slot(k, d), sem, side).wait_send()

    for q in range(units):
        for i in range(1, tps):
            send_hidden(q, i).wait_send()
    for k in pieces:
        sent(k, z, in_sem)

    @pl.when(end)
    def _():
        for p in range(PIECES):
            token_copy(x_hbm, tp, p, 0, inner).wait_send()
        for k in downs:
            for p in range(positions):
                sent(k, p, side_sem)

    @pl.when(jnp.logical_not(end))
    def _():
        for p in range(PIECES):
            for kind in range(2):
                token_copy(guest, tp, p, kind, side).wait_send()
            token_copy(guest, tp, p, 2, side).wait_send()
        for q in range(units):
            send_back(q).wait_send()
        for k in pieces:
            sent(k, z + out, in_sem)
            for p in range(positions):
                sent(k, p, side_sem)
        for k in downs:
            sent(k, z, out_sem)
            sent(k, z - out, out_sem)
            sent(k, far, out_sem)


def streamed(groups, tps, tokens, gain, router, routes, w_gate, w_up, w_down):
    rows, depth = tokens.shape
    experts, shard, width = w_gate.shape
    down_rows, cols = w_down.shape[1:]
    positions = groups // CORES
    half = width // HALVES
    if down_rows != half or half % 128:
        return gathered(tokens, gain, router, routes, w_gate, w_up, w_down)
    hbm = pl.BlockSpec(memory_space=pltpu.HBM)
    units = experts * HALVES
    pieces = 2 * units + experts * CUTS
    dma = pltpu.SemaphoreType.DMA
    return pl.pallas_call(
        functools.partial(kernel, groups, tps),
        out_shape=pltpu.VMEM((rows, cols), jnp.bfloat16),
        in_specs=[hbm] * 7,
        out_specs=pl.BlockSpec(memory_space=pltpu.VMEM),
        scratch_shapes=[
            pltpu.VMEM((rows, depth), jnp.bfloat16),
            pltpu.VMEM((rows, depth), jnp.bfloat16),
            pltpu.VMEM((rows, depth), jnp.bfloat16),
            pltpu.VMEM((units, 2, groups, shard, half), jnp.bfloat16),
            pltpu.VMEM((experts, groups, down_rows, cols), jnp.bfloat16),
            pltpu.VMEM((units, tps, rows, half), jnp.bfloat16),
            pltpu.VMEM((units, rows, half), jnp.bfloat16),
            pltpu.VMEM((rows, router.shape[1]), jnp.float32),
            pltpu.VMEM((rows, cols), jnp.float32),
            pltpu.VMEM((1, depth), jnp.float32),
            pltpu.VMEM((router.shape[1], depth), jnp.float32),
            pltpu.VMEM((routes.shape[1], rows), jnp.int32),
            dma((4,)),
            dma((pieces,)),
            dma((pieces, groups)),
            dma((pieces, positions)),
            dma((pieces, positions)),
            dma((pieces, positions)),
            dma((units, tps - 1)),
            dma((units, tps)),
            dma((3, PIECES)),
            dma((tps, PIECES)),
            dma((units,)),
            dma((units,)),
        ],
        compiler_params=pltpu.CompilerParams(
            collective_id=0, has_side_effects=True, vmem_limit_bytes=60 * 1024 * 1024
        ),
    )(tokens, gain.reshape(1, -1), router.T, routes.T, w_gate, w_up, w_down)


def solution(mesh):
    groups, tps = mesh.shape["dp"], mesh.shape["tp"]
    fits = groups == 4 * CORES and tps == 4
    body = functools.partial(streamed, groups, tps) if fits else gathered
    return jax.shard_map(
        body,
        mesh=mesh,
        in_specs=(
            P("dp", None),
            P(),
            P(),
            P("dp", None),
            P(None, "dp", "tp"),
            P(None, "dp", "tp"),
            P(None, "dp", "tp"),
        ),
        out_specs=P("dp", "tp"),
        check_vma=False,
    )
```

time: 96.8 us -> 88.6 us (0.915)
  Pallas kernels: 94.4 us -> 87.4 us
  local copies, waits for them, and re-layouts: 2.26 us -> 0.97 us
    pallas_call x1, Pallas kernels: 94.4 us -> 87.4 us  [streamed(): pl.pallas_call(functools.partial(kernel, groups, tps), out_shape=pltpu.VM...]
    unnamed x1, local copies, waits for them, and re-layouts: 2.26 us -> 0.97 us
where the time goes in v1:
time: 88.6 us; the launch traced here: 88.4 us
  Pallas kernels  87.4 us (99%)
  local copies, waits for them, and re-layouts  0.97 us (1%)
    pallas_call x1, Pallas kernels, streamed(): pl.pallas_call(functools.partial(kernel, groups, tps), out_shape=pltpu.VM...  87.4 us

profile of v1, /device:TPU:0, one launch (start us, length us, event | category | flops | bytes accessed | tf_op | source)
XLA Modules:
  0.0 88.4 jit_solution(12534326232503849322)
XLA Ops:
  0.0 87.4 %shard_map.73 = bf16[512,1024]{1,0:T(8,128)(2,1)S(1)} custom-call(bf16[512,4096]{1,0:T(8,128)(2,1)} %x_hbm.1, f32[1,4096]{1,0:T(1,128)} %bitcast.4, f32[8,4096]{1,0:T(8,128)} %bitcast.3, s32[2,512]{1,0:T(2,128)} %bitcast.5, bf16[2,512,256]{2,1,0:T(8,128)(2,1)} %wg_hbm.1, bf16[2,512,256]{2,1,0:T(8,128)(2,1)} %wu_hbm.1, bf16[2,128,1024]{2,1,0:T(8,128)(2,1)} %wd_hbm.1), custom_call_target="tpu_custom_call" | custom-call | tf_op jit(solution)/shard_map/pallas_call | solution.py:439
  87.5 1.0 %copy.9 = bf16[512,1024]{1,0:T(8,128)(2,1)} copy(bf16[512,1024]{1,0:T(8,128)(2,1)S(1)} %shard_map.73) | data formatting | bytes 2097152
